TPU v7x, 32 devices: a whole 2x2x4 slice. The times are simulated.
32 devices in a mesh: mrow: 2 (over y), pcol: 16 (over z, x, core).
Axes of the slice: x: 2, y: 2, z: 4, core: 2. Of those that a mesh axis runs over, the one named last changes fastest.
Arguments:
- snapshots: bfloat16 [7424, 4096], P('mrow', 'pcol'), may hold values from -16 to 16
- area_weight: float32 [4096], P('pcol'), may hold values from 0.2 to 1
Outputs:
- gram_tiles: float32 [2, 16, 1722368], P('mrow', 'pcol')
All inputs are finite; a program needn't handle non-finite values.
Results may differ from a plain program's by a relative error of at most 0.0003.
Values may be sent and summed in bfloat16 or wider, within the bound.
A program may use at most 128 MiB of HBM per device.

v0:
```python
import jax
import jax.numpy as jnp
from jax import lax
from jax.sharding import PartitionSpec as P

MEMBERS = 7424


def from_root(value, axis, root):
    mine = lax.axis_index(axis) == root
    return lax.psum(jnp.where(mine, value, jnp.zeros_like(value)), axis)


def local(snapshots, area_weight):
    member_rows = snapshots.shape[0]
    ratio = lax.axis_size("pcol") // lax.axis_size("mrow")
    tile = member_rows // ratio
    local_sum = jnp.sum(snapshots.astype(jnp.float32), axis=0)
    ens_mean = lax.psum(local_sum, "mrow") / MEMBERS
    anomaly = (
        (snapshots.astype(jnp.float32) - ens_mean[None, :]) * jnp.sqrt(area_weight)[None, :]
    ).astype(jnp.bfloat16)
    contract = (((1,), (1,)), ((), ()))
    column_index = lax.axis_index("pcol")
    offset = column_index % ratio * tile
    root = column_index // ratio
    row_block = lax.all_gather(anomaly, "pcol", axis=1, tiled=True)
    picked = lax.dynamic_slice_in_dim(row_block, offset, tile, 0)
    col_block = from_root(picked, "mrow", root)
    gram = lax.dot_general(row_block, col_block, contract, preferred_element_type=jnp.float32)
    gram = gram / (MEMBERS - 1)
    return gram.reshape(1, 1, member_rows * tile)


def solution(mesh):
    placed = (P("mrow", "pcol"), P("pcol"))
    return jax.shard_map(
        local, mesh=mesh, in_specs=placed, out_specs=P("mrow", "pcol", None), check_vma=False
    )
```

profile of v0, /device:TPU:27, one launch (start us, length us, event | category | flops | bytes accessed | tf_op | source)
XLA Modules:
  0.0 338.9 jit_solution(11401928215586227479)
XLA Ops:
  6.5 0.0 all-gather.2.cloned.1.call-start
  6.5 0.7 sqrt.3
  7.2 2.0 convert_reduce_fusion
  9.3 3.8 %psum.14 = f32[256]{0:T(256)S(1)} all-reduce(f32[256]{0:T(256)S(1)} %convert_reduce_fusion), channel_id=1, replica_groups=mesh['mrow'=2,'pcol'=16] {'mrow'}, use_global_device_ids=true, to_apply=%region_1.0 | all-reduce | flops 256 | bytes 2048 | tf_op jit(solution)/shard_map/psum | solution.py:19
  13.0 3.3 fusion.1
  16.3 0.0 all-gather.2.cloned.1.call-update
  16.3 0.0 all-reduce.2.cloned.1.call-start
  16.4 160.1 %all-gather.2.cloned.1.call-done = bf16[3712,4096]{1,0:T(8,128)(2,1)} async-done(((bf16[3712,256]{1,0:T(8,128)(2,1)}), bf16[3712,4096]{1,0:T(8,128)(2,1)}) %all-gather.2.cloned.1.call-update) | async-done | bytes 30408720 | tf_op jit(solution)/shard_map/all_gather | solution.py:27
  176.5 4.9 %dynamic-slice_select_fusion = bf16[464,4096]{1,0:T(8,128)(2,1)} fusion(bf16[3712,4096]{1,0:T(8,128)(2,1)} %all-gather.2.cloned.1.call-done, s32[]{:T(128)S(6)} %select_n.25, pred[]{:T(512)S(6)} %eq.5), kind=kLoop, calls=%fused_computation.5 | loop fusion | flops 1900544 | bytes 7602181 | tf_op jit(solution)/shard_map/jit(_where)/select_n | solution.py:11
  181.4 0.0 all-reduce.2.cloned.1.call-update
  181.5 100.6 %all-reduce.2.cloned.1.call-done = bf16[464,4096]{1,0:T(8,128)(2,1)} async-done(((bf16[464,4096]{1,0:T(8,128)(2,1)}), bf16[464,4096]{1,0:T(8,128)(2,1)}) %all-reduce.2.cloned.1.call-update) | async-done | bytes 3801104 | tf_op jit(solution)/shard_map/psum | solution.py:11
  282.1 21.7 %convolution_multiply_fusion = f32[3712,464]{0,1:T(8,128)} fusion(bf16[3712,4096]{1,0:T(8,128)(2,1)} %all-gather.2.cloned.1.call-done, bf16[464,4096]{1,0:T(8,128)(2,1)} %all-reduce.2.cloned.1.call-done), kind=kOutput, calls=%fused_computation | convolution fusion | flops 14111361024 | bytes 41099264 | tf_op jit(solution)/shard_map/dot_general | solution.py:30
  303.9 8.5 %copy.3 = f32[3712,464]{1,0:T(8,128)} copy(f32[3712,464]{0,1:T(8,128)} %convolution_multiply_fusion) | data formatting | bytes 13778944 | tf_op jit(solution)/shard_map/div | solution.py:31
  312.3 19.7 %reshape.5 = f32[1,1,1722368]{2,1,0:T(1,128)} reshape(f32[3712,464]{1,0:T(8,128)} %copy.3) | data formatting | bytes 13778944 | tf_op jit(solution)/shard_map/reshape | solution.py:32
  (1 shorter events, 0.0 us)
Async XLA Ops:
  6.5 170.0 %all-gather.2.cloned.1.call-start = ((), (), s32[]{:S(2)}) async-start(), calls=%async_computation | async-start | bytes 32309248 | tf_op jit(solution)/shard_map/all_gather | solution.py:27
  16.3 265.8 %all-reduce.2.cloned.1.call-start = ((), (), s32[]{:S(2)}) async-start(), calls=%async_computation.1 | async-start | bytes 7602176 | tf_op jit(solution)/shard_map/psum | solution.py:11
Sparse Core Ops, SparseCore 0:
  16.4 160.0 all-gather.1
  181.6 100.4 all-reduce.1
where the time goes:
time: 341 us; the launch traced here: 339 us
  waiting for transfers between devices  261 us (77%)
  local copies, waits for them, and re-layouts  28.8 us (8%)
  matrix products  21.7 us (6%)
  between operations  13.4 us (4%)
  other arithmetic  10.2 us (3%)
  blocking collectives  3.78 us (1%)
    all_gather x1, waiting for transfers between devices, local(): row_block = lax.all_gather(anomaly, 'pcol', axis=1, tiled=True)  160 us
    psum x1, waiting for transfers between devices, from_root(): return lax.psum(jnp.where(mine, value, jnp.zeros_like(value)), axis)  101 us
    dot_general x1, matrix products, local(): lax.dot_general(row_block, col_block, contract, preferred_element_type=jn...  21.7 us
    reshape x1, local copies, waits for them, and re-layouts, local(): return gram.reshape(1, 1, member_rows * tile)  19.7 us
    div x1, local copies, waits for them, and re-layouts, local(): gram = gram / (MEMBERS - 1)  8.46 us
  transfers between devices with their start and end apart: 2, of which 2 were waited for; matrix products, arithmetic and copies ran while one was open for 0% of the time, Pallas kernels for 0%

commit v1 on v0

v1 whole, which is shorter than its diff:
```python
import functools

import jax
import jax.numpy as jnp
from jax import lax
from jax.experimental import pallas as pl
from jax.experimental.pallas import tpu as pltpu
from jax.sharding import PartitionSpec as P

MEMBERS = 7424
MESH = pl.DeviceIdType.MESH


def gather_gram(n_row, n_col, chunks, tile, a_ref, out_ref, full, cols, in_sem, recv, send, col_recv, col_send):
    rows, depth = a_ref.shape
    length = n_col // 4
    size = rows // chunks
    span = cols.shape[1]
    i = lax.axis_index("mrow")
    me = lax.axis_index("pcol")
    core = lax.rem(me, 2)
    side = lax.rem(me // 2, 2)
    line = me // 4
    ratio = n_col // n_row
    root = me // ratio
    offset = lax.rem(me, ratio) * tile
    aligned = pl.multiple_of(offset // 16 * 16, 16)
    my_chunk = aligned // size

    def index(where, which, own):
        return (where * 2 + which) * 2 + own

    up, down = index(line + 1, side, core), index(line - 1, side, core)
    across, sibling = index(line, 1 - side, core), index(line, side, 1 - core)
    has_up, has_down = line + 1 < length, line >= 1
    peers = [lax.rem(i + step, n_row) for step in range(1, n_row)]
    owns_cols = root == i

    barrier = pltpu.get_barrier_semaphore()

    def greet(row, col):
        pl.semaphore_signal(barrier, inc=1, device_id=(row, col), device_id_type=MESH)

    load = pltpu.make_async_copy(a_ref, full.at[me], in_sem)
    load.start()
    pl.when(has_up)(lambda: greet(i, up))
    pl.when(has_down)(lambda: greet(i, down))
    greet(i, across)
    greet(i, sibling)
    for peer in peers:
        greet(peer, me)
    out_ref[...] = jnp.zeros_like(out_ref)
    load.wait()
    pl.semaphore_wait(barrier, 2 + len(peers) + has_up.astype(jnp.int32) + has_down.astype(jnp.int32))

    def part(s, k):
        return full.at[s, pl.ds(pl.multiple_of(k * size, 16), size)]

    def copy(s, k, way, target):
        return pltpu.make_async_remote_copy(
            src_ref=part(s, k), dst_ref=part(s, k), send_sem=send.at[way, s], recv_sem=recv.at[s, k],
            device_id=(i, target), device_id_type=MESH,
        )

    def col_copy(s, n):
        return pltpu.make_async_remote_copy(
            src_ref=full.at[s, pl.ds(aligned, span)], dst_ref=cols.at[s], send_sem=col_send.at[n],
            recv_sem=col_recv.at[s], device_id=(peers[n], me), device_id_type=MESH,
        )

    def arrived(s, k):
        pltpu.make_async_copy(part(s, k), part(s, k), recv.at[s, k]).wait()

    def share(s, k):
        copy(s, k, 3, sibling).start()

    def to_peers(s, k):
        @pl.when(jnp.logical_and(owns_cols, k == my_chunk))
        def _():
            for n in range(len(peers)):
                col_copy(s, n).start()

    def go_up(s, k):
        pl.when(has_up)(lambda: copy(s, k, 0, up).start())

    def go_down(s, k):
        pl.when(has_down)(lambda: copy(s, k, 1, down).start())

    def own(k, _):
        copy(me, k, 2, across).start()
        go_up(me, k)
        go_down(me, k)
        share(me, k)
        to_peers(me, k)
        return 0

    lax.fori_loop(0, chunks, own, 0)
    arrived(across, 0)
    go_up(across, 0)
    go_down(across, 0)
    share(across, 0)
    to_peers(across, 0)

    def valid(sign, distance):
        place = line + sign * distance
        inside = jnp.logical_and(place >= 0, place < length)
        far = distance >= 1 if sign > 0 else distance >= 0
        return jnp.logical_and(inside, far)

    def step(d, _):
        def from_sibling(k):
            for sign in (-1, 1):
                for which, distance in ((side, d), (1 - side, d - 1)):
                    @pl.when(valid(sign, distance))
                    def _():
                        s = index(line + sign * distance, which, 1 - core)
                        arrived(s, k)
                        to_peers(s, k)

        def piece(k, _):
            for sign, forward in ((-1, go_up), (1, go_down)):
                @pl.when(valid(sign, d))
                def _():
                    s = index(line + sign * d, side, core)
                    arrived(s, k)
                    forward(s, k)
                    pl.when(k >= 1)(lambda: copy(s, k, 2, across).start())
                    share(s, k)
                    to_peers(s, k)

                    @pl.when(k == 0)
                    def _():
                        t = index(line + sign * d, 1 - side, core)
                        arrived(t, 0)
                        forward(t, 0)
                        share(t, 0)
                        to_peers(t, 0)

            for sign in (-1, 1):
                @pl.when(jnp.logical_and(valid(sign, d - 1), k >= 1))
                def _():
                    s = index(line + sign * (d - 1), 1 - side, core)
                    arrived(s, k)
                    share(s, k)
                    to_peers(s, k)

            pl.when(k >= 1)(lambda: from_sibling(k - 1))
            multiply(d - 1, k)
            return 0

        lax.fori_loop(0, chunks, piece, 0)
        from_sibling(chunks - 1)
        for sign in (-1, 1):
            for which, distance in ((side, d), (1 - side, d - 1)):
                for other in (core, 1 - core):
                    pl.when(valid(sign, distance))(
                        lambda: take_cols(index(line + sign * distance, which, other))
                    )
        return 0

    def take_cols(s):
        @pl.when(owns_cols)
        def _():
            cols[s] = full[s, pl.ds(aligned, span), :]

        @pl.when(jnp.logical_not(owns_cols))
        def _():
            pltpu.make_async_copy(cols.at[s], cols.at[s], col_recv.at[s]).wait()

    def multiply(d, k):
        row = pl.ds(pl.multiple_of(k * size, 16), size)

        def one(n, _):
            sign = 1 - 2 * (n // 4)
            cross = lax.rem(n // 2, 2)
            distance = d - cross
            place = line + sign * distance
            good = jnp.logical_and(place >= 0, place < length)
            good = jnp.logical_and(good, distance >= n // 4)
            good = jnp.logical_and(good, distance >= 0)

            @pl.when(good)
            def _():
                s = index(place, lax.rem(side + cross, 2), lax.rem(n, 2))
                right = cols[s]
                if span != tile:
                    right = jnp.where(offset == aligned, right[:tile], right[span - tile:])
                out_ref[row, :] += lax.dot_general(
                    full[s, row, :], right, (((1,), (1,)), ((), ())), preferred_element_type=jnp.float32
                )

            return 0

        lax.fori_loop(0, 8, one, 0)

    def ready_own(k, _):
        s = index(line, side, 1 - core)
        arrived(s, k)
        to_peers(s, k)
        return 0

    lax.fori_loop(0, chunks, ready_own, 0)
    take_cols(me)
    take_cols(sibling)
    lax.fori_loop(1, length + 1, step, 0)

    def last(k, _):
        multiply(length, k)
        return 0

    lax.fori_loop(0, chunks, last, 0)
    out_ref[...] = out_ref[...] / (MEMBERS - 1)

    def sent(s, way, first, count):
        ref = full.at[s, pl.ds(first * size, count * size)]
        pltpu.make_async_copy(ref, ref, send.at[way, s]).wait()

    def drain(place, _):
        straight, cross = index(place, side, core), index(place, 1 - side, core)
        sent(straight, 3, 0, chunks)
        sent(cross, 3, 0, chunks)
        pl.when(place == line)(lambda: sent(straight, 2, 0, chunks))
        pl.when(place != line)(lambda: sent(straight, 2, 1, chunks - 1))

        @pl.when(jnp.logical_and(has_up, place <= line))
        def _():
            sent(straight, 0, 0, chunks)
            sent(cross, 0, 0, 1)

        @pl.when(jnp.logical_and(has_down, place >= line))
        def _():
            sent(straight, 1, 0, chunks)
            sent(cross, 1, 0, 1)

        return 0

    lax.fori_loop(0, length, drain, 0)

    @pl.when(owns_cols)
    def _():
        for n in range(len(peers)):
            pltpu.make_async_copy(cols, cols, col_send.at[n]).wait()


def local(n_row, n_col, snapshots, area_weight):
    rows, depth = snapshots.shape
    tile = rows * n_row // n_col
    chunks = 8
    while rows % (16 * chunks):
        chunks //= 2
    span = tile + tile % 16
    local_sum = jnp.sum(snapshots.astype(jnp.float32), axis=0)
    ens_mean = lax.psum(local_sum, "mrow") / MEMBERS
    anomaly = (
        (snapshots.astype(jnp.float32) - ens_mean[None, :]) * jnp.sqrt(area_weight)[None, :]
    ).astype(jnp.bfloat16)
    gram = pl.pallas_call(
        functools.partial(gather_gram, n_row, n_col, chunks, tile),
        out_shape=jax.ShapeDtypeStruct((rows, tile), jnp.float32),
        in_specs=[pl.BlockSpec(memory_space=pl.ANY)],
        out_specs=pl.BlockSpec(memory_space=pltpu.VMEM),
        scratch_shapes=[
            pltpu.VMEM((n_col, rows, depth), jnp.bfloat16),
            pltpu.VMEM((n_col, span, depth), jnp.bfloat16),
            pltpu.SemaphoreType.DMA,
            pltpu.SemaphoreType.DMA((n_col, chunks)),
            pltpu.SemaphoreType.DMA((4, n_col)),
            pltpu.SemaphoreType.DMA((n_col,)),
            pltpu.SemaphoreType.DMA((max(n_row - 1, 1),)),
        ],
        compiler_params=pltpu.CompilerParams(
            collective_id=0, has_side_effects=True, vmem_limit_bytes=60 * 2**20
        ),
        name="gather_gram",
    )(anomaly)
    return gram.reshape(1, 1, rows * tile)


def solution(mesh):
    placed = (P("mrow", "pcol"), P("pcol"))
    return jax.shard_map(
        functools.partial(local, mesh.shape["mrow"], mesh.shape["pcol"]),
        mesh=mesh, in_specs=placed, out_specs=P("mrow", "pcol", None), check_vma=False,
    )
```

time: 341 us -> 217 us (0.64)
  waiting for transfers between devices: 261 us -> 0 us
  Pallas kernels: 0 us -> 187 us
  matrix products: 21.7 us -> 0 us
  between operations: 13.4 us -> 0.01 us
  local copies, waits for them, and re-layouts: 28.8 us -> 20.4 us
  other arithmetic: 10.2 us -> 5.29 us
    pallas_call x0 -> x1, Pallas kernels: none -> 187 us  [local(): pl.pallas_call(functools.partial(gather_gram, n_row, n_col, chunks, tile)...]
    all_gather x1 -> x0, waiting for transfers between devices: 160 us -> none  [local(): row_block = lax.all_gather(anomaly, 'pcol', axis=1, tiled=True)]
    psum x1 -> x0, waiting for transfers between devices: 101 us -> none  [from_root(): return lax.psum(jnp.where(mine, value, jnp.zeros_like(value)), axis)]
    dot_general x1 -> x0, matrix products: 21.7 us -> none  [local(): lax.dot_general(row_block, col_block, contract, preferred_element_type=jn...]
    div x1 -> x0, local copies, waits for them, and re-layouts: 8.46 us -> none  [local(): gram = gram / (MEMBERS - 1)]
    select_n x1 -> x0, other arithmetic: 4.91 us -> none  [from_root(): return lax.psum(jnp.where(mine, value, jnp.zeros_like(value)), axis)]
  transfers between devices with their start and end apart: 2 -> 0, of which waited for: 2 -> 0; matrix products, arithmetic and copies ran while one was open for 0% -> 0% of each run, Pallas kernels for 0% -> 0%
where the time goes in v1:
time: 217 us; the launch traced here: 216 us
  Pallas kernels  187 us (86%)
  local copies, waits for them, and re-layouts  20.4 us (9%)
  other arithmetic  5.29 us (2%)
  blocking collectives  3.78 us (2%)
    pallas_call x1, Pallas kernels, local(): pl.pallas_call(functools.partial(gather_gram, n_row, n_col, chunks, tile)...  187 us
    reshape x1, local copies, waits for them, and re-layouts, local(): return gram.reshape(1, 1, rows * tile)  19.7 us

profile of v1, /device:TPU:27, one launch (start us, length us, event | category | flops | bytes accessed | tf_op | source)
XLA Modules:
  0.0 216.3 jit_solution(13757752888682666631)
XLA Ops:
  0.0 0.7 sqrt.3
  0.7 2.0 convert_reduce_fusion
  2.7 3.8 %psum.7 = f32[256]{0:T(256)S(1)} all-reduce(f32[256]{0:T(256)S(1)} %convert_reduce_fusion), channel_id=1, replica_groups=mesh['mrow'=2,'pcol'=16] {'mrow'}, use_global_device_ids=true, to_apply=%region_1.0 | all-reduce | flops 256 | bytes 2048 | tf_op jit(solution)/shard_map/psum | solution.py:253
  6.5 3.3 %fusion.1.a_ref = bf16[3712,256]{1,0:T(8,128)(2,1)} fusion(bf16[3712,256]{1,0:T(8,128)(2,1)} %param.2, f32[256]{0:T(256)S(1)} %sqrt.3, f32[256]{0:T(256)S(1)} %broadcast_multiply_fusion), kind=kLoop, calls=%fused_computation.3 | loop fusion | flops 3801088 | bytes 3803136 | tf_op jit(solution)/shard_map/convert_element_type | solution.py:256
  9.8 186.8 %gather_gram.1 = f32[3712,464]{1,0:T(8,128)} custom-call(bf16[3712,256]{1,0:T(8,128)(2,1)} %fusion.1.a_ref), custom_call_target="tpu_custom_call" | custom-call | tf_op jit(solution)/shard_map/gather_gram/pallas_call | solution.py:257
  196.6 19.7 %reshape.5 = f32[1,1,1722368]{2,1,0:T(1,128)} reshape(f32[3712,464]{1,0:T(8,128)} %gather_gram.1) | data formatting | bytes 13778944 | tf_op jit(solution)/shard_map/reshape | solution.py:276
  (1 shorter events, 0.0 us)

commit v2 on v1

--- a/solution.py
+++ b/solution.py
@@ -8,11 +8,15 @@
 from jax.sharding import PartitionSpec as P
 
 MEMBERS = 7424
+MAX_CHUNKS = 32
 MESH = pl.DeviceIdType.MESH
 
 
-def gather_gram(n_row, n_col, chunks, tile, a_ref, out_ref, full, cols, in_sem, recv, send, col_recv, col_send):
-    rows, depth = a_ref.shape
+def gather_gram(
+    n_row, n_col, chunks, early, pieces, tile, x_ref, weight_ref, out_ref, full, cols, sums, recv, send, col_recv, col_send,
+    sum_recv, sum_send,
+):
+    rows, depth = x_ref.shape
     length = n_col // 4
     size = rows // chunks
     span = cols.shape[1]
@@ -25,7 +29,8 @@
     root = me // ratio
     offset = lax.rem(me, ratio) * tile
     aligned = pl.multiple_of(offset // 16 * 16, 16)
-    my_chunk = aligned // size
+    my_chunk = (aligned + span - 1) // size
+    stride = chunks // pieces
 
     def index(where, which, own):
         return (where * 2 + which) * 2 + own
@@ -41,16 +46,18 @@
     def greet(row, col):
         pl.semaphore_signal(barrier, inc=1, device_id=(row, col), device_id_type=MESH)
 
-    load = pltpu.make_async_copy(a_ref, full.at[me], in_sem)
-    load.start()
     pl.when(has_up)(lambda: greet(i, up))
     pl.when(has_down)(lambda: greet(i, down))
     greet(i, across)
     greet(i, sibling)
     for peer in peers:
         greet(peer, me)
-    out_ref[...] = jnp.zeros_like(out_ref)
-    load.wait()
+
+    def add_up(k, total):
+        block = x_ref[pl.ds(pl.multiple_of(k * size, 16), size), :].astype(jnp.float32)
+        return total + jnp.sum(block.reshape(size // 8, 8, depth), axis=0)
+
+    sums[i] = lax.fori_loop(0, chunks, add_up, jnp.zeros((8, depth), jnp.float32))
     pl.semaphore_wait(barrier, 2 + len(peers) + has_up.astype(jnp.int32) + has_down.astype(jnp.int32))
 
     def part(s, k):
@@ -86,7 +93,26 @@
     def go_down(s, k):
         pl.when(has_down)(lambda: copy(s, k, 1, down).start())
 
+    def sum_copy(n):
+        return pltpu.make_async_remote_copy(
+            src_ref=sums.at[i], dst_ref=sums.at[i], send_sem=sum_send.at[n], recv_sem=sum_recv.at[i],
+            device_id=(peers[n], me), device_id_type=MESH,
+        )
+
+    for n in range(len(peers)):
+        sum_copy(n).start()
+    out_ref[...] = jnp.zeros_like(out_ref)
+    for peer in peers:
+        pltpu.make_async_copy(sums.at[peer], sums.at[peer], sum_recv.at[peer]).wait()
+    mean = jnp.sum(jnp.sum(sums[...], axis=0), axis=0, keepdims=True) / MEMBERS
+    root_weight = jnp.sqrt(weight_ref[...])
+
+    def center(k):
+        row = pl.ds(pl.multiple_of(k * size, 16), size)
+        full[me, row, :] = ((x_ref[row, :].astype(jnp.float32) - mean) * root_weight).astype(jnp.bfloat16)
+
     def own(k, _):
+        pl.when(k + 1 < chunks)(lambda: center(k + 1))
         copy(me, k, 2, across).start()
         go_up(me, k)
         go_down(me, k)
@@ -94,12 +120,18 @@
         to_peers(me, k)
         return 0
 
+    center(0)
     lax.fori_loop(0, chunks, own, 0)
-    arrived(across, 0)
-    go_up(across, 0)
-    go_down(across, 0)
-    share(across, 0)
-    to_peers(across, 0)
+
+    def cross_first(k, _):
+        arrived(across, k)
+        go_up(across, k)
+        go_down(across, k)
+        share(across, k)
+        to_peers(across, k)
+        return 0
+
+    lax.fori_loop(0, early, cross_first, 0)
 
     def valid(sign, distance):
         place = line + sign * distance
@@ -124,20 +156,20 @@
                     s = index(line + sign * d, side, core)
                     arrived(s, k)
                     forward(s, k)
-                    pl.when(k >= 1)(lambda: copy(s, k, 2, across).start())
+                    pl.when(k >= early)(lambda: copy(s, k, 2, across).start())
                     share(s, k)
                     to_peers(s, k)
 
-                    @pl.when(k == 0)
+                    @pl.when(k < early)
                     def _():
                         t = index(line + sign * d, 1 - side, core)
-                        arrived(t, 0)
-                        forward(t, 0)
-                        share(t, 0)
-                        to_peers(t, 0)
+                        arrived(t, k)
+                        forward(t, k)
+                        share(t, k)
+                        to_peers(t, k)
 
             for sign in (-1, 1):
-                @pl.when(jnp.logical_and(valid(sign, d - 1), k >= 1))
+                @pl.when(jnp.logical_and(valid(sign, d - 1), k >= early))
                 def _():
                     s = index(line + sign * (d - 1), 1 - side, core)
                     arrived(s, k)
@@ -145,7 +177,11 @@
                     to_peers(s, k)
 
             pl.when(k >= 1)(lambda: from_sibling(k - 1))
-            multiply(d - 1, k)
+
+            @pl.when(jnp.logical_and(lax.rem(k, stride) == stride - 1, k // stride < pieces))
+            def _():
+                multiply(d - 1, k // stride)
+
             return 0
 
         lax.fori_loop(0, chunks, piece, 0)
@@ -168,7 +204,7 @@
             pltpu.make_async_copy(cols.at[s], cols.at[s], col_recv.at[s]).wait()
 
     def multiply(d, k):
-        row = pl.ds(pl.multiple_of(k * size, 16), size)
+        row = pl.ds(pl.multiple_of(k * (rows // pieces), 16), rows // pieces)
 
         def one(n, _):
             sign = 1 - 2 * (n // 4)
@@ -185,9 +221,12 @@
                 right = cols[s]
                 if span != tile:
                     right = jnp.where(offset == aligned, right[:tile], right[span - tile:])
-                out_ref[row, :] += lax.dot_general(
+                product = lax.dot_general(
                     full[s, row, :], right, (((1,), (1,)), ((), ())), preferred_element_type=jnp.float32
                 )
+                for b in range(out_ref.shape[0]):
+                    width = min(128, tile - b * 128)
+                    out_ref[b, row, :width] += product[:, b * 128:b * 128 + width]
 
             return 0
 
@@ -208,8 +247,7 @@
         multiply(length, k)
         return 0
 
-    lax.fori_loop(0, chunks, last, 0)
-    out_ref[...] = out_ref[...] / (MEMBERS - 1)
+    lax.fori_loop(0, pieces, last, 0)
 
     def sent(s, way, first, count):
         ref = full.at[s, pl.ds(first * size, count * size)]
@@ -220,17 +258,17 @@
         sent(straight, 3, 0, chunks)
         sent(cross, 3, 0, chunks)
         pl.when(place == line)(lambda: sent(straight, 2, 0, chunks))
-        pl.when(place != line)(lambda: sent(straight, 2, 1, chunks - 1))
+        pl.when(place != line)(lambda: sent(straight, 2, early, chunks - early))
 
         @pl.when(jnp.logical_and(has_up, place <= line))
         def _():
             sent(straight, 0, 0, chunks)
-            sent(cross, 0, 0, 1)
+            sent(cross, 0, 0, early)
 
         @pl.when(jnp.logical_and(has_down, place >= line))
         def _():
             sent(straight, 1, 0, chunks)
-            sent(cross, 1, 0, 1)
+            sent(cross, 1, 0, early)
 
         return 0
 
@@ -241,39 +279,81 @@
         for n in range(len(peers)):
             pltpu.make_async_copy(cols, cols, col_send.at[n]).wait()
 
+    for n in range(len(peers)):
+        pltpu.make_async_copy(sums.at[i], sums.at[i], sum_send.at[n]).wait()
+
+
+def flatten(tile, group, gram_ref, flat_ref):
+    many = gram_ref.shape[1] // group
+    wide = group * tile // 128
+    scale = jnp.float32(1.0 / (MEMBERS - 1))
+    for s in range(wide):
+        parts = []
+        at = s * 128
+        while at < (s + 1) * 128:
+            r, c = at // tile, at % tile
+            count = min(tile - c, (s + 1) * 128 - at)
+            parts.append((r, c, count, at - s * 128))
+            at += count
+        lane = lax.broadcasted_iota(jnp.int32, (many, 128), 1)
+        value = None
+        for r, c, count, to in parts:
+            shift = (to - c) % 128
+            here = gram_ref[c // 128, pl.ds(r, many, stride=group), :]
+            here = pltpu.roll(here, shift, 1) if shift else here
+            if c % 128 + count > 128:
+                then = gram_ref[c // 128 + 1, pl.ds(r, many, stride=group), :]
+                then = pltpu.roll(then, shift, 1) if shift else then
+                here = jnp.where(lane < to + 128 - c % 128, here, then)
+            value = here if value is None else jnp.where(lane < to, value, here)
+        flat_ref[pl.ds(s, many, stride=wide), :] = value * scale
+
 
 def local(n_row, n_col, snapshots, area_weight):
     rows, depth = snapshots.shape
     tile = rows * n_row // n_col
-    chunks = 8
-    while rows % (16 * chunks):
-        chunks //= 2
+    units = rows // 16
+    chunks = max(n for n in range(1, MAX_CHUNKS + 1) if units % n == 0)
+    pieces = max(n for n in range(1, 9) if units % n == 0)
+    early = max(1, round(chunks / 6))
     span = tile + tile % 16
-    local_sum = jnp.sum(snapshots.astype(jnp.float32), axis=0)
-    ens_mean = lax.psum(local_sum, "mrow") / MEMBERS
-    anomaly = (
-        (snapshots.astype(jnp.float32) - ens_mean[None, :]) * jnp.sqrt(area_weight)[None, :]
-    ).astype(jnp.bfloat16)
+    blocks = -(-tile // 128)
     gram = pl.pallas_call(
-        functools.partial(gather_gram, n_row, n_col, chunks, tile),
-        out_shape=jax.ShapeDtypeStruct((rows, tile), jnp.float32),
-        in_specs=[pl.BlockSpec(memory_space=pl.ANY)],
+        functools.partial(gather_gram, n_row, n_col, chunks, early, pieces, tile),
+        out_shape=jax.ShapeDtypeStruct((blocks, rows, 128), jnp.float32),
+        in_specs=[pl.BlockSpec(memory_space=pltpu.VMEM)] * 2,
         out_specs=pl.BlockSpec(memory_space=pltpu.VMEM),
         scratch_shapes=[
             pltpu.VMEM((n_col, rows, depth), jnp.bfloat16),
             pltpu.VMEM((n_col, span, depth), jnp.bfloat16),
-            pltpu.SemaphoreType.DMA,
+            pltpu.VMEM((n_row, 8, depth), jnp.float32),
             pltpu.SemaphoreType.DMA((n_col, chunks)),
             pltpu.SemaphoreType.DMA((4, n_col)),
             pltpu.SemaphoreType.DMA((n_col,)),
+            pltpu.SemaphoreType.DMA((max(n_row - 1, 1),)),
+            pltpu.SemaphoreType.DMA((n_row,)),
             pltpu.SemaphoreType.DMA((max(n_row - 1, 1),)),
         ],
         compiler_params=pltpu.CompilerParams(
             collective_id=0, has_side_effects=True, vmem_limit_bytes=60 * 2**20
         ),
         name="gather_gram",
-    )(anomaly)
-    return gram.reshape(1, 1, rows * tile)
+    )(snapshots, area_weight.reshape(1, depth))
+    group = 8
+    while group * tile % 128:
+        group *= 2
+    groups = rows // group
+    block = 16 if groups % 16 == 0 else groups
+    wide = group * tile // 128
+    flat = pl.pallas_call(
+        functools.partial(flatten, tile, group),
+        grid=(groups // block,),
+        out_shape=jax.ShapeDtypeStruct((groups * wide, 128), jnp.float32),
+        in_specs=[pl.BlockSpec((blocks, block * group, 128), lambda n: (0, n, 0))],
+        out_specs=pl.BlockSpec((block * wide, 128), lambda n: (n, 0)),
+        name="flatten",
+    )(gram)
+    return flat.reshape(1, 1, rows * tile)
 
 
 def solution(mesh):

time: 217 us -> 225 us (1.037)
  Pallas kernels: 187 us -> 224 us
  local copies, waits for them, and re-layouts: 20.4 us -> 0 us
  other arithmetic: 5.29 us -> 0 us
  blocking collectives: 3.78 us -> 0 us
    pallas_call x1 -> x2, Pallas kernels: 187 us -> 224 us  [the longest x1 205 us: local(): pl.pallas_call(functools.partial(gather_gram, n_row, n_col, chunks, early...]
    reshape x1 -> x0, local copies, waits for them, and re-layouts: 19.7 us -> none  [local(): return gram.reshape(1, 1, rows * tile)]
    psum x1 -> x0, blocking collectives: 3.78 us -> none  [local(): ens_mean = lax.psum(local_sum, 'mrow') / MEMBERS]
    convert_element_type x1 -> x0, other arithmetic: 3.26 us -> none  [local(): anomaly = ((snapshots.astype(jnp.float32) - ens_mean[None, :]) * jnp.sqrt...]
where the time goes in v2:
time: 225 us; the launch traced here: 224 us
  Pallas kernels  224 us (100%)
    pallas_call x1, Pallas kernels, local(): pl.pallas_call(functools.partial(gather_gram, n_row, n_col, chunks, early...  205 us
    pallas_call x1, Pallas kernels, local(): pl.pallas_call(functools.partial(flatten, tile, group), grid=(groups // b...  19.3 us

profile of v2, /device:TPU:27, one launch (start us, length us, event | category | flops | bytes accessed | tf_op | source)
XLA Modules:
  0.0 224.4 jit_solution(5922895456323685265)
XLA Ops:
  0.0 205.0 %gather_gram.1.gram_ref = f32[4,3712,128]{2,1,0:T(8,128)} custom-call(bf16[3712,256]{1,0:T(8,128)(2,1)} %x_ref.1, f32[1,256]{1,0:T(1,128)} %bitcast.2), custom_call_target="tpu_custom_call" | custom-call | tf_op jit(solution)/shard_map/gather_gram/pallas_call | solution.py:321
  205.0 19.3 %flatten.1 = f32[13456,128]{1,0:T(8,128)} custom-call(f32[4,3712,128]{2,1,0:T(8,128)} %gather_gram.1.gram_ref), custom_call_target="tpu_custom_call" | custom-call | tf_op jit(solution)/shard_map/flatten/pallas_call | solution.py:348

commit v3 on v2

--- a/solution.py
+++ b/solution.py
@@ -8,7 +8,7 @@
 from jax.sharding import PartitionSpec as P
 
 MEMBERS = 7424
-MAX_CHUNKS = 32
+MAX_CHUNKS = 8
 MESH = pl.DeviceIdType.MESH
 
 
@@ -343,7 +343,7 @@
     while group * tile % 128:
         group *= 2
     groups = rows // group
-    block = 16 if groups % 16 == 0 else groups
+    block = max((n for n in range(8, 257, 8) if groups % n == 0), default=groups)
     wide = group * tile // 128
     flat = pl.pallas_call(
         functools.partial(flatten, tile, group),

time: 225 us -> 196 us (0.87)
  Pallas kernels: 224 us -> 196 us
    pallas_call x1, Pallas kernels: 205 us -> 188 us  [local(): pl.pallas_call(functools.partial(gather_gram, n_row, n_col, chunks, early...]
    pallas_call x1, Pallas kernels: 19.3 us -> 7.35 us  [local(): pl.pallas_call(functools.partial(flatten, tile, group), grid=(groups // b...]
where the time goes in v3:
time: 196 us
  Pallas kernels  196 us (100%)
    pallas_call x1, Pallas kernels, local(): pl.pallas_call(functools.partial(gather_gram, n_row, n_col, chunks, early...  188 us
    pallas_call x1, Pallas kernels, local(): pl.pallas_call(functools.partial(flatten, tile, group), grid=(groups // b...  7.35 us

profile of v3, /device:TPU:27, one launch (start us, length us, event | category | flops | bytes accessed | tf_op | source)
XLA Modules:
  0.0 195.5 jit_solution(17472959858717898632)
XLA Ops:
  0.0 188.2 %gather_gram.1.gram_ref = f32[4,3712,128]{2,1,0:T(8,128)} custom-call(bf16[3712,256]{1,0:T(8,128)(2,1)} %x_ref.1, f32[1,256]{1,0:T(1,128)} %bitcast.2), custom_call_target="tpu_custom_call" | custom-call | tf_op jit(solution)/shard_map/gather_gram/pallas_call | solution.py:321
  188.2 7.4 %flatten.1 = f32[13456,128]{1,0:T(8,128)} custom-call(f32[4,3712,128]{2,1,0:T(8,128)} %gather_gram.1.gram_ref), custom_call_target="tpu_custom_call" | custom-call | tf_op jit(solution)/shard_map/flatten/pallas_call | solution.py:348
